TPU v7x, 32 devices: a whole 2x2x4 slice. The times are simulated.
32 devices in a mesh: dp: 8 (over z, x), mp: 4 (over y, core).
Axes of the slice: x: 2, y: 2, z: 4, core: 2. Of those that a mesh axis runs over, the one named last changes fastest.
Arguments:
- acts: bfloat16 [1, 16384, 4096], P(None, 'dp'), may hold values from -64 to 64
- out_grads: bfloat16 [1, 16384, 4096], P(None, 'dp', 'mp'), may hold values from -80 to 80
- clip_bound: float32 [1], replicated, may hold values from 163840 to 491520
- noise: float32 [1, 4096, 4096], P(None, 'dp', 'mp'), may hold values from -6 to 6
Outputs:
- update: float32 [1, 4096, 4096], P(None, 'dp', 'mp')
All inputs are finite; a program needn't handle non-finite values.
Results may differ from a plain program's by a relative error of at most 0.0017.
Values may be sent and summed in bfloat16 or wider, within the bound.
A program may use at most 128 MiB of HBM per device.

v0:
```python
import math
import jax
import jax.numpy as jnp
from jax import lax
from jax.sharding import PartitionSpec as P

SEQ = 512


def ghost_partial(act_block, grad_block, examples):
    act_seq = act_block.reshape(examples, SEQ, act_block.shape[1])
    grad_seq = grad_block.reshape(examples, SEQ, grad_block.shape[1])
    gram_act = jnp.einsum("etd,esd->ets", act_seq, act_seq, preferred_element_type=jnp.float32)
    gram_grad = jnp.einsum("etd,esd->ets", grad_seq, grad_seq, preferred_element_type=jnp.float32)
    return jnp.sum(gram_act * gram_grad, axis=(1, 2))


def scale_grads(grad_block, norm_sq, bound, examples):
    clip = jnp.minimum(1.0, bound / jnp.sqrt(norm_sq + 1e-06))
    factor = clip / bound
    grad_seq = grad_block.reshape(examples, SEQ, grad_block.shape[1]).astype(jnp.float32)
    scaled = (grad_seq * factor[:, None, None]).astype(jnp.bfloat16)
    return scaled.reshape(grad_block.shape)


def on_device(acts, out_grads, clip_bound, noise):
    examples = acts.shape[1] // SEQ
    model_width = acts.shape[2]
    batch_total = examples * lax.axis_size("dp")
    out_factor = model_width / math.sqrt(batch_total)
    act_block = acts[0]
    norm_sq = lax.psum(ghost_partial(act_block, out_grads[0], examples), "mp")
    scaled = scale_grads(out_grads[0], norm_sq, clip_bound[0], examples)

    def term_rows(begin_row, row_count, act_block=act_block, scaled=scaled):
        return lax.dot_general(
            act_block, scaled, (((0,), (0,)), ((), ())), preferred_element_type=jnp.float32
        )

    summed = lax.psum_scatter(
        term_rows(jnp.int32(0), model_width // lax.axis_size("dp") * lax.axis_size("dp")),
        "dp",
        scatter_dimension=0,
        tiled=True,
    )
    updates = [summed * out_factor + noise[0]]
    return jnp.stack(updates)


def solution(mesh):
    placed = (P(None, "dp", None), P(None, "dp", "mp"), P(), P(None, "dp", "mp"))
    return jax.shard_map(
        on_device, mesh=mesh, in_specs=placed, out_specs=P(None, "dp", "mp"), check_vma=False
    )
```

profile of v0, /device:TPU:0, one launch (start us, length us, event | category | flops | bytes accessed | tf_op | source)
XLA Modules:
  0.0 358.5 jit_solution(12628637458226172755)
XLA Ops:
  6.5 0.0 reduce-scatter.2.cloned.1.call-start
  6.5 7.8 %fusion.9 = f32[4,512,512]{2,1,0:T(8,128)} fusion(bf16[4,512,1024]{2,1,0:T(8,128)(2,1)} %bitcast.29), kind=kOutput, calls=%fused_computation.11 | convolution fusion | flops 2147483648 | bytes 8388608 | tf_op jit(solution)/shard_map/etd,esd->ets/dot_general | solution.py:14
  14.3 16.9 %multiply_reduce_fusion = f32[4]{0:T(128)S(1)} fusion(f32[4,512,512]{2,1,0:T(8,128)} %fusion.9, bf16[4,512,4096]{2,1,0:T(8,128)(2,1)} %bitcast.28), kind=kOutput, calls=%fused_computation.6 | convolution fusion | flops 8592031744 | bytes 20971536 | tf_op jit(solution)/shard_map/etd,esd->ets/dot_general | solution.py:13
  31.2 8.6 %psum.7 = f32[4]{0:T(128)S(1)} all-reduce(f32[4]{0:T(128)S(1)} %multiply_reduce_fusion), channel_id=1, replica_groups=mesh['dp'=8,'mp'=4] {'mp'}, use_global_device_ids=true, to_apply=%region_1.0 | all-reduce | flops 4 | bytes 32 | tf_op jit(solution)/shard_map/psum | solution.py:32
  40.4 0.1 broadcast_bitcast_fusion
  40.5 24.2 %fusion.2 = f32[4096,1024]{0,1:T(8,128)} fusion(bf16[1,2048,4096]{2,1,0:T(8,128)(2,1)} %param.4, bf16[1,2048,1024]{2,1,0:T(8,128)(2,1)} %param.5, f32[2048]{0:T(1024)S(1)} %bitcast.27), kind=kOutput, calls=%fused_computation.2 | convolution fusion | flops 17186160640 | bytes 37756928 | tf_op jit(solution)/shard_map/dot_general | solution.py:36
  64.7 0.0 reduce-scatter.2.cloned.1.call-update
  64.7 1.9 copy.5
  66.7 278.7 %reduce-scatter.2.cloned.1.call-done = f32[512,1024]{0,1:T(8,128)} async-done(((f32[4096,1024]{0,1:T(8,128)}), f32[512,1024]{0,1:T(8,128)}) %reduce-scatter.2.cloned.1.call-update) | async-done | bytes 2097168 | tf_op jit(solution)/shard_map/reduce_scatter | solution.py:40
  345.4 3.4 fusion.8
  348.8 2.9 copy.6
  (2 shorter events, 0.0 us)
Async XLA Ops:
  6.5 338.8 %reduce-scatter.2.cloned.1.call-start = ((), (), s32[]{:S(2)}) async-start(), calls=%async_computation.1 | async-start | bytes 18874368 | tf_op jit(solution)/shard_map/reduce_scatter | solution.py:40
Sparse Core Ops, SparseCore 0:
  64.9 280.4 reduce-scatter.1
where the time goes:
time: 359 us
  waiting for transfers between devices  279 us (78%)
  matrix products  48.9 us (14%)
  between operations  14.1 us (4%)
  blocking collectives  8.55 us (2%)
  local copies, waits for them, and re-layouts  4.88 us (1%)
    reduce_scatter x1, waiting for transfers between devices, on_device(): lax.psum_scatter(term_rows(jnp.int32(0), model_width // lax.axis_size('dp...  279 us
    dot_general x1, matrix products, term_rows(): lax.dot_general(act_block, scaled, (((0,), (0,)), ((), ())), preferred_el...  24.2 us
    dot_general x1, matrix products, ghost_partial(): jnp.einsum('etd,esd->ets', act_seq, act_seq, preferred_element_type=jnp.f...  16.9 us
    psum x1, blocking collectives, on_device(): norm_sq = lax.psum(ghost_partial(act_block, out_grads[0], examples), 'mp')  8.55 us
    dot_general x1, matrix products, ghost_partial(): jnp.einsum('etd,esd->ets', grad_seq, grad_seq, preferred_element_type=jnp...  7.76 us
  transfers between devices with their start and end apart: 1, of which 1 were waited for; matrix products, arithmetic and copies ran while one was open for 1% of the time, Pallas kernels for 0%

commit v1 on v0

--- a/solution.py
+++ b/solution.py
@@ -29,7 +29,8 @@
     batch_total = examples * lax.axis_size("dp")
     out_factor = model_width / math.sqrt(batch_total)
     act_block = acts[0]
-    norm_sq = lax.psum(ghost_partial(act_block, out_grads[0], examples), "mp")
+    panel = ghost_partial(act_block, out_grads[0], examples)
+    norm_sq = jnp.sum(lax.all_gather(panel, axis_name="mp"), 0)
     scaled = scale_grads(out_grads[0], norm_sq, clip_bound[0], examples)
 
     def term_rows(begin_row, row_count, act_block=act_block, scaled=scaled):

time: 359 us -> 360 us (level)
    psum x1 -> x0, blocking collectives: 8.55 us -> none  [on_device(): norm_sq = lax.psum(ghost_partial(act_block, out_grads[0], examples), 'mp')]
    unnamed x0 -> x1, blocking collectives: none -> 8.54 us
where the time goes in v1:
time: 360 us
  waiting for transfers between devices  279 us (78%)
  matrix products  48.9 us (14%)
  between operations  14.7 us (4%)
  blocking collectives  8.54 us (2%)
  local copies, waits for them, and re-layouts  5.8 us (2%)
    reduce_scatter x1, waiting for transfers between devices, on_device(): lax.psum_scatter(term_rows(jnp.int32(0), model_width // lax.axis_size('dp...  279 us
    dot_general x1, matrix products, term_rows(): lax.dot_general(act_block, scaled, (((0,), (0,)), ((), ())), preferred_el...  24.2 us
    dot_general x1, matrix products, ghost_partial(): jnp.einsum('etd,esd->ets', act_seq, act_seq, preferred_element_type=jnp.f...  16.9 us
    unnamed x1, blocking collectives  8.54 us
    dot_general x1, matrix products, ghost_partial(): jnp.einsum('etd,esd->ets', grad_seq, grad_seq, preferred_element_type=jnp...  7.76 us
  transfers between devices with their start and end apart: 1, of which 1 were waited for; matrix products, arithmetic and copies ran while one was open for 1% of the time, Pallas kernels for 0%

profile of v1, /device:TPU:0, one launch (start us, length us, event | category | flops | bytes accessed | tf_op | source)
XLA Modules:
  0.0 360.2 jit_solution(17711162212659652402)
XLA Ops:
  6.5 0.0 reduce-scatter.2.cloned.1.call-start
  6.5 7.8 %fusion.9 = f32[4,512,512]{2,1,0:T(8,128)} fusion(bf16[4,512,1024]{2,1,0:T(8,128)(2,1)} %bitcast.30), kind=kOutput, calls=%fused_computation.11 | convolution fusion | flops 2147483648 | bytes 8388608 | tf_op jit(solution)/shard_map/etd,esd->ets/dot_general | solution.py:14
  14.3 0.0 copy-start
  14.3 16.9 %multiply_reduce_fusion = f32[4]{0:T(128)S(1)} fusion(f32[4,512,512]{2,1,0:T(8,128)} %fusion.9, bf16[4,512,4096]{2,1,0:T(8,128)(2,1)} %bitcast.29), kind=kOutput, calls=%fused_computation.6 | convolution fusion | flops 8592031744 | bytes 20971536 | tf_op jit(solution)/shard_map/etd,esd->ets/dot_general | solution.py:13
  31.2 0.0 copy-done
  31.2 0.6 dynamic-slice
  32.4 0.2 dynamic-update-slice
  32.7 8.5 %all-reduce = f32[16]{0:T(128)S(1)} all-reduce(f32[16]{0:T(128)S(1)} %dynamic-update-slice), channel_id=2, replica_groups=mesh['dp'=8,'mp'=4] {'mp'}, use_global_device_ids=true, to_apply=%add | all-reduce | flops 16 | bytes 128
  41.2 0.1 reshape.18
  42.0 0.1 broadcast_bitcast_fusion
  42.1 24.2 %fusion.2 = f32[4096,1024]{0,1:T(8,128)} fusion(bf16[1,2048,4096]{2,1,0:T(8,128)(2,1)} %param.4, bf16[1,2048,1024]{2,1,0:T(8,128)(2,1)} %param.5, f32[2048]{0:T(1024)S(1)} %bitcast.28), kind=kOutput, calls=%fused_computation.2 | convolution fusion | flops 17186160640 | bytes 37756928 | tf_op jit(solution)/shard_map/dot_general | solution.py:37
  66.3 0.0 reduce-scatter.2.cloned.1.call-update
  66.3 1.9 copy.5
  68.3 278.7 %reduce-scatter.2.cloned.1.call-done = f32[512,1024]{0,1:T(8,128)} async-done(((f32[4096,1024]{0,1:T(8,128)}), f32[512,1024]{0,1:T(8,128)}) %reduce-scatter.2.cloned.1.call-update) | async-done | bytes 2097168 | tf_op jit(solution)/shard_map/reduce_scatter | solution.py:41
  347.0 3.4 fusion.8
  350.4 2.9 copy.6
  (4 shorter events, 0.0 us)
Async XLA Ops:
  6.5 340.5 %reduce-scatter.2.cloned.1.call-start = ((), (), s32[]{:S(2)}) async-start(), calls=%async_computation.1 | async-start | bytes 18874368 | tf_op jit(solution)/shard_map/reduce_scatter | solution.py:41
  14.3 16.9 %copy-start = (u32[32]{0:T(128)S(1)}, u32[32]{0:T(128)}, u32[]{:S(2)}) copy-start(u32[32]{0:T(128)} %constant.10) | copy-start | bytes 388
Sparse Core Ops, SparseCore 0:
  66.5 280.5 reduce-scatter.1
